TPU v7x, 32 devices: a whole 2x2x4 slice. The times are simulated.
32 devices in a mesh: group: 2 (over y), seq: 4 (over z), tensor: 4 (over x, core).
Axes of the slice: x: 2, y: 2, z: 4, core: 2. Of those that a mesh axis runs over, the one named last changes fastest.
Arguments:
- query: bfloat16 [16, 7168], P(('group', 'seq'), 'tensor'), parts along dimension 0, may hold values from -5 to 5
- key_cache: bfloat16 [32, 256, 7168], P(('group', 'seq'), None, 'tensor'), parts along dimension 0, may hold values from -5 to 5
- value_cache: bfloat16 [32, 256, 7168], P(('group', 'seq'), None, 'tensor'), parts along dimension 0, may hold values from -6 to 6
- alibi_slopes: float32 [56], P('tensor'), may hold values from 0 to 1, as said below
- block_seq: int32 [32], P(('group', 'seq')), parts along dimension 0, may hold values from 0 to 7, as said below
- block_pos: int32 [32], P(('group', 'seq')), parts along dimension 0, may hold values from 0 to 2, as said below
- lengths: int32 [16], P('group'), parts along dimension 0, may hold values from 1 to 768, as said below
- out_weight: bfloat16 [7168, 14336], P('tensor', 'seq'), may hold values from -0.5 to 0.5
Outputs:
- mixed: bfloat16 [16, 14336], P(('group', 'tensor'), 'seq'), parts along dimension 0
There are 2 independent parts, one for each index of `group`. A program takes and returns all parts, laid end to end along the dimension named above; an argument that names none is the same for every part. Nothing has to cross between parts.
Inputs may be any that keep to these rules, and one draw needn't show every extreme that they name: `block_seq`: every sequence owns at least one block and at most 3; the blocks of sequence s have block_pos 0 to n_s - 1, each once. block_pos of a block is below the number of blocks its sequence owns. `lengths`: A sequence that owns n blocks has a length above 256 * (n - 1) and at most 256 * n. `alibi_slopes`: positive slopes.
All inputs are finite; a program needn't handle non-finite values.
Results may differ from a plain program's by a relative error of at most 0.0054.
Values may be sent and summed in bfloat16 or wider, within the bound.
No kernel may reach another device: no remote copies, remote signals or barrier semaphores. Data moves between devices by JAX's collectives and lax.ppermute only.
A program may use at most 64 MiB of HBM per device.

v0:
```python
import math
import jax
import jax.numpy as jnp
from jax import lax
from jax.sharding import PartitionSpec as P


def local(query, key_cache, value_cache, alibi_slopes, block_seq, block_pos, lengths, out_weight):
    heads = alibi_slopes.shape[0]
    features = query.shape[1]
    head_size = features // heads
    blocks_here = key_cache.shape[0]
    block_len = key_cache.shape[1]
    seq_count = lengths.shape[0]
    scale = 1.0 / math.sqrt(head_size)
    whole_query = lax.all_gather(query, "seq", axis=0, tiled=True)
    query_rows = jnp.take(whole_query, block_seq, axis=0).reshape(blocks_here, heads, head_size)
    keys = key_cache.reshape(blocks_here, block_len, heads, head_size)
    values = value_cache.reshape(blocks_here, block_len, heads, head_size)
    scores = (
        jnp.einsum("bthd,bhd->bht", keys, query_rows, preferred_element_type=jnp.float32) * scale
    )
    owner_length = lengths[block_seq]
    placed = block_pos[:, None] * block_len + jnp.arange(block_len, dtype=jnp.int32)[None, :]
    live = (placed < owner_length[:, None])[:, None, :]
    distance = (owner_length[:, None] - 1 - placed).astype(jnp.float32)
    scores = scores - alibi_slopes[None, :, None] * distance[:, None, :]
    scores = jnp.where(live, scores, -1e30)
    block_top = jnp.max(scores, axis=2)
    weights = jnp.where(live, jnp.exp(scores - block_top[:, :, None]), 0.0)
    block_total = jnp.sum(weights, axis=2)
    block_acc = jnp.einsum(
        "bht,bthd->bhd", weights.astype(jnp.bfloat16), values, preferred_element_type=jnp.float32
    )
    seq_ids = jnp.arange(seq_count, dtype=jnp.int32)
    owned = (block_seq[None, :] == seq_ids[:, None])[:, :, None]
    local_top = jnp.max(jnp.where(owned, block_top[None], -1e30), axis=1)
    factor = jnp.where(owned, jnp.exp(block_top[None] - local_top[:, None, :]), 0.0)
    local_total = jnp.sum(factor * block_total[None], axis=1)
    local_acc = jnp.einsum("sbh,bhd->shd", factor, block_acc, precision=lax.Precision.HIGHEST)
    tops, totals, accs = (
        lax.all_to_all(local_top[None], "seq", split_axis=1, concat_axis=0, tiled=True),
        lax.all_to_all(local_total[None], "seq", split_axis=1, concat_axis=0, tiled=True),
        lax.all_to_all(local_acc[None], "seq", split_axis=1, concat_axis=0, tiled=True),
    )
    best = jnp.max(tops, axis=0)
    scaling = jnp.exp(tops - best[None])
    home_total = jnp.sum(totals * scaling, axis=0)
    home_acc = jnp.sum(accs * scaling[..., None], axis=0)
    mine = (
        (home_acc / home_total[:, :, None])
        .astype(jnp.bfloat16)
        .reshape(home_acc.shape[0], features)
    )
    attention = lax.all_gather(mine, "seq", axis=0, tiled=True)
    mixed = lax.psum_scatter(
        jnp.dot(attention, out_weight, preferred_element_type=jnp.float32),
        "tensor",
        scatter_dimension=0,
        tiled=True,
    )
    return mixed.astype(jnp.bfloat16)


def solution(mesh):
    placed = (
        P(("group", "seq"), "tensor"),
        P(("group", "seq"), None, "tensor"),
        P(("group", "seq"), None, "tensor"),
        P("tensor"),
        P(("group", "seq")),
        P(("group", "seq")),
        P("group"),
        P("tensor", "seq"),
    )
    return jax.shard_map(
        local, mesh=mesh, in_specs=placed, out_specs=P(("group", "tensor"), "seq"), check_vma=False
    )
```

profile of v0, /device:TPU:0, one launch (start us, length us, event | category | flops | bytes accessed | tf_op | source)
XLA Modules:
  0.0 95.4 jit_solution(14486349411866468453)
XLA Ops:
  0.0 0.0 copy-start
  0.0 0.7 compare_select_fusion
  0.7 0.7 compare_and_fusion
  1.3 0.7 iota_compare_fusion
  2.1 0.0 copy-done
  2.1 0.6 gather_fusion
  2.7 0.7 broadcast_add_fusion
  3.4 0.1 fusion.16
  3.5 0.1 subtract_convert_fusion
  3.5 15.1 %all-gather = bf16[4,2,1792]{2,1,0:T(2,128)(2,1)S(1)} all-gather(bf16[1,2,1792]{2,1,0:T(2,128)(2,1)} %bitcast.41), channel_id=1, replica_groups=mesh['group'=2,'seq'=4,'tensor'=4] {'seq'}, dimensions={0}, use_global_device_ids=true | all-gather | bytes 35840 | tf_op jit(solution)/shard_map/all_gather | solution.py:16
  18.6 0.6 gather_fusion.1
  19.2 6.0 %copy.49 = bf16[4,256,1792]{1,2,0:T(8,128)(2,1)} copy(bf16[4,256,1792]{2,1,0:T(8,128)(2,1)} %param.9) | data formatting | bytes 7340032 | tf_op args[1]
  25.2 0.0 copy-start.1
  25.2 0.1 select_bitcast_fusion
  25.3 2.6 %fusion.9 = f32[4,14,1,256]{3,2,1,0:T(1,128)S(1)} fusion(bf16[4,256,14,128]{1,3,2,0:T(8,128)(2,1)} %bitcast.33, bf16[4,14,128,1]{2,1,0,3:T(8,128)(2,1)S(1)} %select_bitcast_fusion), kind=kOutput, calls=%fused_computation.16 | convolution fusion | flops 3670016 | bytes 3741696 | tf_op jit(solution)/shard_map/bthd,bhd->bht/dot_general | solution.py:21
  27.9 0.0 copy-done.1
  27.9 0.2 fusion.18
  28.0 0.1 select_reduce_fusion
  28.1 0.7 copy.54
  28.8 4.7 %all-to-all-start.1 = ((f32[1,8,14]{2,0,1:T(1,128)}), f32[1,8,14]{2,0,1:T(1,128)S(1)}, u32[]{:S(2)}, u32[]{:S(2)}) async-start(f32[1,8,14]{2,0,1:T(1,128)} %copy.54), calls=%async_computation.1 | async-start | bytes 8192 | tf_op jit(solution)/shard_map/all_to_all | solution.py:42
  33.6 0.2 fusion.4
  33.7 0.1 multiply_reduce_fusion.1
  33.8 6.0 %copy.50 = bf16[4,256,1792]{1,2,0:T(8,128)(2,1)} copy(bf16[4,256,1792]{2,1,0:T(8,128)(2,1)} %param.10) | data formatting | bytes 7340032 | tf_op args[2]
  39.8 0.0 copy-start.2
  39.8 3.1 %fusion.2 = f32[4,14,1,128]{3,2,1,0:T(1,128)S(1)} fusion(bf16[4,256,14,128]{1,3,2,0:T(8,128)(2,1)} %bitcast.34, bf16[4,14,256,1]{2,0,1,3:T(4,128)(2,1)S(1)} %get-tuple-element.10), kind=kOutput, calls=%fused_computation.6 | convolution fusion | flops 3670016 | bytes 3727360 | tf_op jit(solution)/shard_map/bht,bthd->bhd/dot_general | solution.py:32
  42.9 0.4 convolution_bitcast_fusion
  43.3 0.7 copy.57
  44.0 0.0 all-to-all-done.1
  44.0 5.1 %all-to-all-start.2 = ((f32[1,8,14]{2,0,1:T(1,128)}), f32[1,8,14]{2,0,1:T(1,128)S(1)}, u32[]{:S(2)}, u32[]{:S(2)}) async-start(f32[1,8,14]{2,0,1:T(1,128)} %copy.57), calls=%async_computation.2 | async-start | bytes 8192 | tf_op jit(solution)/shard_map/all_to_all | solution.py:43
  49.1 0.7 copy.51
  49.7 0.0 copy-done.2
  49.7 0.6 dynamic-slice
  51.0 3.7 %all-to-all-done.2 = f32[1,8,14]{2,0,1:T(1,128)S(1)} async-done(((f32[1,8,14]{2,0,1:T(1,128)}), f32[1,8,14]{2,0,1:T(1,128)S(1)}, u32[]{:S(2)}, u32[]{:S(2)}) %all-to-all-start.2) | async-done | bytes 480 | tf_op jit(solution)/shard_map/all_to_all | solution.py:43
  54.6 3.3 %all-to-all-start = ((f32[1,8,14,128]{3,0,2,1:T(1,128)}), f32[1,8,14,128]{3,0,2,1:T(1,128)S(1)}, u32[]{:S(2)}, u32[]{:S(2)}) async-start(f32[1,8,14,128]{3,0,2,1:T(1,128)} %copy.51), calls=%async_computation | async-start | bytes 114688 | tf_op jit(solution)/shard_map/all_to_all | solution.py:44
  58.0 0.1 copy.55
  58.1 0.1 copy.58
  58.2 5.5 %all-to-all-done = f32[1,8,14,128]{3,0,2,1:T(1,128)S(1)} async-done(((f32[1,8,14,128]{3,0,2,1:T(1,128)}), f32[1,8,14,128]{3,0,2,1:T(1,128)S(1)}, u32[]{:S(2)}, u32[]{:S(2)}) %all-to-all-start) | async-done | bytes 57376 | tf_op jit(solution)/shard_map/all_to_all | solution.py:44
  63.6 0.1 multiply_reduce_fusion
  63.8 0.1 fusion.15
  63.9 13.2 %all-gather.1 = bf16[4,2,1792]{2,1,0:T(2,128)(2,1)S(1)} all-gather(bf16[1,2,1792]{2,1,0:T(2,128)(2,1)S(1)} %fusion.15), channel_id=1, replica_groups=mesh['group'=2,'seq'=4,'tensor'=4] {'seq'}, dimensions={0}, use_global_device_ids=true | all-gather | bytes 35840 | tf_op jit(solution)/shard_map/all_gather | solution.py:55
  77.1 6.4 %fusion.20 = f32[8,3584]{1,0:T(8,128)S(1)} fusion(bf16[8,1792]{1,0:T(8,128)(2,1)S(1)} %reshape.152, bf16[1792,3584]{1,0:T(8,128)(2,1)} %param.15), kind=kOutput, calls=%fused_computation.41 | convolution fusion | flops 102760448 | bytes 12988416 | tf_op jit(solution)/shard_map/dot_general | solution.py:57
  83.5 11.3 %all-reduce = bf16[8,3584]{1,0:T(8,128)(2,1)S(1)} all-reduce(f32[8,3584]{1,0:T(8,128)S(1)} %fusion.20), channel_id=2, replica_groups=mesh['group'=2,'seq'=4,'tensor'=4] {'tensor'}, use_global_device_ids=true, to_apply=%region_7.8.clone | all-reduce | flops 28672 | bytes 172032
  94.7 0.6 dynamic-slice_convert_fusion
  (7 shorter events, 0.1 us)
Async XLA Ops:
  0.0 2.1 %copy-start = (s32[8]{0:T(128)S(1)}, s32[8]{0:T(128)}, u32[]{:S(2)}) copy-start(s32[8]{0:T(128)} %param.14) | copy-start | bytes 100
  25.2 2.7 %copy-start.1 = (f32[14]{0:T(128)S(1)}, f32[14]{0:T(128)}, u32[]{:S(2)}) copy-start(f32[14]{0:T(128)} %param.11) | copy-start | bytes 172
  28.8 15.2 %all-to-all-start.1 = ((f32[1,8,14]{2,0,1:T(1,128)}), f32[1,8,14]{2,0,1:T(1,128)S(1)}, u32[]{:S(2)}, u32[]{:S(2)}) async-start(f32[1,8,14]{2,0,1:T(1,128)} %copy.54), calls=%async_computation.1 | async-start | bytes 8192 | tf_op jit(solution)/shard_map/all_to_all | solution.py:42
  39.8 9.9 %copy-start.2 = (u32[32]{0:T(128)S(1)}, u32[32]{0:T(128)}, u32[]{:S(2)}) copy-start(u32[32]{0:T(128)} %constant.39) | copy-start | bytes 388
  44.0 10.7 %all-to-all-start.2 = ((f32[1,8,14]{2,0,1:T(1,128)}), f32[1,8,14]{2,0,1:T(1,128)S(1)}, u32[]{:S(2)}, u32[]{:S(2)}) async-start(f32[1,8,14]{2,0,1:T(1,128)} %copy.57), calls=%async_computation.2 | async-start | bytes 8192 | tf_op jit(solution)/shard_map/all_to_all | solution.py:43
  54.6 9.0 %all-to-all-start = ((f32[1,8,14,128]{3,0,2,1:T(1,128)}), f32[1,8,14,128]{3,0,2,1:T(1,128)S(1)}, u32[]{:S(2)}, u32[]{:S(2)}) async-start(f32[1,8,14,128]{3,0,2,1:T(1,128)} %copy.51), calls=%async_computation | async-start | bytes 114688 | tf_op jit(solution)/shard_map/all_to_all | solution.py:44
where the time goes:
time: 96.1 us; the launch traced here: 95.4 us
  blocking collectives  39.5 us (41%)
  local copies, waits for them, and re-layouts  16.7 us (17%)
  starting transfers between devices  13.1 us (14%)
  matrix products  12.5 us (13%)
  waiting for transfers between devices  9.12 us (9%)
  other arithmetic  3.75 us (4%)
    all_gather x1, blocking collectives, local(): whole_query = lax.all_gather(query, 'seq', axis=0, tiled=True)  15.1 us
    all_gather x1, blocking collectives, local(): attention = lax.all_gather(mine, 'seq', axis=0, tiled=True)  13.2 us
    unnamed x11, local copies, waits for them, and re-layouts  12.6 us
    unnamed x1, blocking collectives  11.3 us
    dot_general x1, matrix products, local(): jnp.dot(attention, out_weight, preferred_element_type=jnp.float32)  6.41 us
    all_to_all x1, waiting for transfers between devices, local(): lax.all_to_all(local_acc[None], 'seq', split_axis=1, concat_axis=0, tiled...  5.46 us
    all_to_all x1, starting transfers between devices, local(): lax.all_to_all(local_total[None], 'seq', split_axis=1, concat_axis=0, til...  5.09 us
    all_to_all x1, starting transfers between devices, local(): lax.all_to_all(local_top[None], 'seq', split_axis=1, concat_axis=0, tiled...  4.74 us
  transfers between devices with their start and end apart: 3, of which 2 were waited for; matrix products, arithmetic and copies ran while one was open for 13% of the time, Pallas kernels for 0%

commit v1 on v0

--- a/solution.py
+++ b/solution.py
@@ -6,6 +6,25 @@
 
 
 def local(query, key_cache, value_cache, alibi_slopes, block_seq, block_pos, lengths, out_weight):
+
+    def do_table_here(unit, chip_axis, d0=0):
+        n_chips = jax.lax.axis_size(chip_axis)
+        block_list = [(q, (q + 1) % n_chips) for q in range(n_chips)]
+        stack_in = [(q, (q - 1) % n_chips) for q in range(n_chips)]
+        y_new, t1 = ([unit], [unit])
+        for _ in range(n_chips // 2):
+            y_new.append(jax.lax.ppermute(y_new[-1], chip_axis, block_list))
+        j = 0
+        while j < (n_chips - 1) // 2:
+            t1.append(jax.lax.ppermute(t1[-1], chip_axis, stack_in))
+            j += 1
+        e_now = jnp.roll(
+            jnp.concatenate([*y_new[::-1], *t1[1:]], d0),
+            (jax.lax.axis_index(chip_axis) - n_chips // 2) * unit.shape[d0],
+            d0,
+        )
+        return e_now
+
     heads = alibi_slopes.shape[0]
     features = query.shape[1]
     head_size = features // heads
@@ -13,7 +32,7 @@
     block_len = key_cache.shape[1]
     seq_count = lengths.shape[0]
     scale = 1.0 / math.sqrt(head_size)
-    whole_query = lax.all_gather(query, "seq", axis=0, tiled=True)
+    whole_query = do_table_here(query, chip_axis="seq")
     query_rows = jnp.take(whole_query, block_seq, axis=0).reshape(blocks_here, heads, head_size)
     keys = key_cache.reshape(blocks_here, block_len, heads, head_size)
     values = value_cache.reshape(blocks_here, block_len, heads, head_size)

time: 96.1 us -> 87.6 us (0.912)
  blocking collectives: 39.5 us -> 24.4 us
  starting transfers between devices: 13.1 us -> 16.9 us
  waiting for transfers between devices: 9.12 us -> 11.7 us
    all_gather x1 -> x0, blocking collectives: 15.1 us -> none  [local(): whole_query = lax.all_gather(query, 'seq', axis=0, tiled=True)]
    ppermute x0 -> x3, starting transfers between devices: none -> 5.14 us  [the longest x2 3.05 us: do_table_here(): y_new.append(jax.lax.ppermute(y_new[-1], chip_axis, block_list))]
    all_to_all x1, starting transfers between devices: 5.09 us -> 3.4 us  [local(): lax.all_to_all(local_total[None], 'seq', split_axis=1, concat_axis=0, til...]
    all_to_all x1, waiting for transfers between devices: 0.01 us -> 1.7 us  [local(): lax.all_to_all(local_top[None], 'seq', split_axis=1, concat_axis=0, tiled...]
    unnamed x11 -> x12, local copies, waits for them, and re-layouts: 12.6 us -> 12.6 us
  transfers between devices with their start and end apart: 3 -> 6, of which waited for: 2 -> 3; matrix products, arithmetic and copies ran while one was open for 13% -> 24% of each run, Pallas kernels for 0% -> 0%
where the time goes in v1:
time: 87.6 us; the launch traced here: 86.8 us
  blocking collectives  24.4 us (28%)
  starting transfers between devices  16.9 us (19%)
  local copies, waits for them, and re-layouts  16.8 us (19%)
  matrix products  12.5 us (14%)
  waiting for transfers between devices  11.7 us (13%)
  other arithmetic  3.76 us (4%)
    all_gather x1, blocking collectives, local(): attention = lax.all_gather(mine, 'seq', axis=0, tiled=True)  13.2 us
    unnamed x12, local copies, waits for them, and re-layouts  12.6 us
    unnamed x1, blocking collectives  11.3 us
    dot_general x1, matrix products, local(): jnp.dot(attention, out_weight, preferred_element_type=jnp.float32)  6.41 us
    all_to_all x1, waiting for transfers between devices, local(): lax.all_to_all(local_acc[None], 'seq', split_axis=1, concat_axis=0, tiled...  5.46 us
    all_to_all x1, starting transfers between devices, local(): lax.all_to_all(local_top[None], 'seq', split_axis=1, concat_axis=0, tiled...  5.08 us
    all_to_all x1, waiting for transfers between devices, local(): lax.all_to_all(local_total[None], 'seq', split_axis=1, concat_axis=0, til...  4.5 us
    all_to_all x1, starting transfers between devices, local(): lax.all_to_all(local_total[None], 'seq', split_axis=1, concat_axis=0, til...  3.4 us
  transfers between devices with their start and end apart: 6, of which 3 were waited for; matrix products, arithmetic and copies ran while one was open for 24% of the time, Pallas kernels for 0%

profile of v1, /device:TPU:0, one launch (start us, length us, event | category | flops | bytes accessed | tf_op | source)
XLA Modules:
  0.0 86.8 jit_solution(4952878045545377944)
XLA Ops:
  0.0 0.0 copy-start
  0.0 3.1 %collective-permute-start = (bf16[2,1792]{1,0:T(2,128)(2,1)}, bf16[2,1792]{1,0:T(2,128)(2,1)S(1)}, u32[]{:S(2)}, u32[]{:S(2)}) collective-permute-start(bf16[2,1792]{1,0:T(2,128)(2,1)} %param.8), channel_id=1, source_target_pairs={{0,4},{4,8},{8,12},{12,0},{1,5},{5,9},{9,13},{13,1},{2,6},{6,10},{... | collective-permute-start | bytes 21512 | tf_op jit(solution)/shard_map/ppermute | solution.py:16
  3.1 2.1 %collective-permute-start.2 = (bf16[2,1792]{1,0:T(2,128)(2,1)}, bf16[2,1792]{1,0:T(2,128)(2,1)S(1)}, u32[]{:S(2)}, u32[]{:S(2)}) collective-permute-start(bf16[2,1792]{1,0:T(2,128)(2,1)} %param.8), channel_id=1, source_target_pairs={{0,12},{4,0},{8,4},{12,8},{1,13},{5,1},{9,5},{13,9},{2,14},{6,2},{... | collective-permute-start | bytes 21512 | tf_op jit(solution)/shard_map/ppermute | solution.py:19
  5.1 0.7 compare_select_fusion
  5.8 0.0 copy-done
  5.8 0.6 gather_fusion
  6.4 0.7 broadcast_add_fusion
  7.1 0.1 fusion.16
  7.2 0.1 subtract_convert_fusion
  7.3 0.7 compare_and_fusion
  7.9 0.0 collective-permute-done
  7.9 0.0 collective-permute-start.1
  7.9 0.7 iota_compare_fusion
  8.7 6.0 %copy.49 = bf16[4,256,1792]{1,2,0:T(8,128)(2,1)} copy(bf16[4,256,1792]{2,1,0:T(8,128)(2,1)} %param.9) | data formatting | bytes 7340032 | tf_op args[1]
  14.7 0.0 copy-start.3
  14.7 0.0 copy-start.1
  14.7 6.0 %copy.50 = bf16[4,256,1792]{1,2,0:T(8,128)(2,1)} copy(bf16[4,256,1792]{2,1,0:T(8,128)(2,1)} %param.10) | data formatting | bytes 7340032 | tf_op args[2]
  20.6 0.0 copy-start.2
  20.6 0.0 copy-done.3
  20.7 0.6 dynamic-slice
  21.9 0.0 collective-permute-done.2
  21.9 0.0 collective-permute-done.1
  21.9 0.0 copy-done.1
  21.9 0.1 concatenate.6
  22.1 0.6 gather_fusion.1
  22.7 0.1 select_bitcast_fusion
  22.7 2.6 %fusion.9 = f32[4,14,1,256]{3,2,1,0:T(1,128)S(1)} fusion(bf16[4,256,14,128]{1,3,2,0:T(8,128)(2,1)} %bitcast.33, bf16[4,14,128,1]{2,1,0,3:T(8,128)(2,1)S(1)} %select_bitcast_fusion), kind=kOutput, calls=%fused_computation.16 | convolution fusion | flops 3670016 | bytes 3741696 | tf_op jit(solution)/shard_map/bthd,bhd->bht/dot_general | solution.py:40
  25.3 0.0 copy-done.2
  25.3 0.2 fusion.18
  25.5 0.2 fusion.4
  25.7 0.1 select_reduce_fusion
  25.8 0.7 copy.54
  26.5 5.1 %all-to-all-start.1 = ((f32[1,8,14]{2,0,1:T(1,128)}), f32[1,8,14]{2,0,1:T(1,128)S(1)}, u32[]{:S(2)}, u32[]{:S(2)}) async-start(f32[1,8,14]{2,0,1:T(1,128)} %copy.54), calls=%async_computation.1 | async-start | bytes 8192 | tf_op jit(solution)/shard_map/all_to_all | solution.py:61
  31.6 3.1 %fusion.2 = f32[4,14,1,128]{3,2,1,0:T(1,128)S(1)} fusion(bf16[4,256,14,128]{1,3,2,0:T(8,128)(2,1)} %bitcast.32, bf16[4,14,256,1]{2,0,1,3:T(4,128)(2,1)S(1)} %get-tuple-element.10), kind=kOutput, calls=%fused_computation.6 | convolution fusion | flops 3670016 | bytes 3727360 | tf_op jit(solution)/shard_map/bht,bthd->bhd/dot_general | solution.py:51
  34.6 0.1 multiply_reduce_fusion.1
  34.8 0.7 copy.57
  35.4 1.7 %all-to-all-done.1 = f32[1,8,14]{2,0,1:T(1,128)S(1)} async-done(((f32[1,8,14]{2,0,1:T(1,128)}), f32[1,8,14]{2,0,1:T(1,128)S(1)}, u32[]{:S(2)}, u32[]{:S(2)}) %all-to-all-start.1) | async-done | bytes 480 | tf_op jit(solution)/shard_map/all_to_all | solution.py:61
  37.1 3.4 %all-to-all-start.2 = ((f32[1,8,14]{2,0,1:T(1,128)}), f32[1,8,14]{2,0,1:T(1,128)S(1)}, u32[]{:S(2)}, u32[]{:S(2)}) async-start(f32[1,8,14]{2,0,1:T(1,128)} %copy.57), calls=%async_computation.2 | async-start | bytes 8192 | tf_op jit(solution)/shard_map/all_to_all | solution.py:62
  40.5 0.4 convolution_bitcast_fusion
  40.9 0.7 copy.51
  41.6 4.5 %all-to-all-done.2 = f32[1,8,14]{2,0,1:T(1,128)S(1)} async-done(((f32[1,8,14]{2,0,1:T(1,128)}), f32[1,8,14]{2,0,1:T(1,128)S(1)}, u32[]{:S(2)}, u32[]{:S(2)}) %all-to-all-start.2) | async-done | bytes 480 | tf_op jit(solution)/shard_map/all_to_all | solution.py:62
  46.1 3.3 %all-to-all-start = ((f32[1,8,14,128]{3,0,2,1:T(1,128)}), f32[1,8,14,128]{3,0,2,1:T(1,128)S(1)}, u32[]{:S(2)}, u32[]{:S(2)}) async-start(f32[1,8,14,128]{3,0,2,1:T(1,128)} %copy.51), calls=%async_computation | async-start | bytes 114688 | tf_op jit(solution)/shard_map/all_to_all | solution.py:63
  49.4 0.1 copy.55
  49.5 0.1 copy.58
  49.6 5.5 %all-to-all-done = f32[1,8,14,128]{3,0,2,1:T(1,128)S(1)} async-done(((f32[1,8,14,128]{3,0,2,1:T(1,128)}), f32[1,8,14,128]{3,0,2,1:T(1,128)S(1)}, u32[]{:S(2)}, u32[]{:S(2)}) %all-to-all-start) | async-done | bytes 57376 | tf_op jit(solution)/shard_map/all_to_all | solution.py:63
  55.1 0.1 multiply_reduce_fusion
  55.2 0.1 fusion.15
  55.3 13.2 %all-gather = bf16[4,2,1792]{2,1,0:T(2,128)(2,1)S(1)} all-gather(bf16[1,2,1792]{2,1,0:T(2,128)(2,1)S(1)} %fusion.15), channel_id=1, replica_groups=mesh['group'=2,'seq'=4,'tensor'=4] {'seq'}, dimensions={0}, use_global_device_ids=true | all-gather | bytes 35840 | tf_op jit(solution)/shard_map/all_gather | solution.py:74
  68.5 6.4 %fusion.20 = f32[8,3584]{1,0:T(8,128)S(1)} fusion(bf16[8,1792]{1,0:T(8,128)(2,1)S(1)} %reshape.150, bf16[1792,3584]{1,0:T(8,128)(2,1)} %param.15), kind=kOutput, calls=%fused_computation.42 | convolution fusion | flops 102760448 | bytes 12988416 | tf_op jit(solution)/shard_map/dot_general | solution.py:76
  74.9 11.3 %all-reduce = bf16[8,3584]{1,0:T(8,128)(2,1)S(1)} all-reduce(f32[8,3584]{1,0:T(8,128)S(1)} %fusion.20), channel_id=2, replica_groups=mesh['group'=2,'seq'=4,'tensor'=4] {'tensor'}, use_global_device_ids=true, to_apply=%region_7.8.clone | all-reduce | flops 28672 | bytes 172032
  86.2 0.6 dynamic-slice_convert_fusion
  (7 shorter events, 0.1 us)
Async XLA Ops:
  0.0 5.8 %copy-start = (s32[8]{0:T(128)S(1)}, s32[8]{0:T(128)}, u32[]{:S(2)}) copy-start(s32[8]{0:T(128)} %param.14) | copy-start | bytes 100
  0.0 7.9 %collective-permute-start = (bf16[2,1792]{1,0:T(2,128)(2,1)}, bf16[2,1792]{1,0:T(2,128)(2,1)S(1)}, u32[]{:S(2)}, u32[]{:S(2)}) collective-permute-start(bf16[2,1792]{1,0:T(2,128)(2,1)} %param.8), channel_id=1, source_target_pairs={{0,4},{4,8},{8,12},{12,0},{1,5},{5,9},{9,13},{13,1},{2,6},{6,10},{... | collective-permute-start | bytes 21512 | tf_op jit(solution)/shard_map/ppermute | solution.py:16
  3.1 18.8 %collective-permute-start.2 = (bf16[2,1792]{1,0:T(2,128)(2,1)}, bf16[2,1792]{1,0:T(2,128)(2,1)S(1)}, u32[]{:S(2)}, u32[]{:S(2)}) collective-permute-start(bf16[2,1792]{1,0:T(2,128)(2,1)} %param.8), channel_id=1, source_target_pairs={{0,12},{4,0},{8,4},{12,8},{1,13},{5,1},{9,5},{13,9},{2,14},{6,2},{... | collective-permute-start | bytes 21512 | tf_op jit(solution)/shard_map/ppermute | solution.py:19
  7.9 14.0 %collective-permute-start.1 = (bf16[2,1792]{1,0:T(2,128)(2,1)S(1)}, bf16[2,1792]{1,0:T(2,128)(2,1)S(1)}, u32[]{:S(2)}, u32[]{:S(2)}) collective-permute-start(bf16[2,1792]{1,0:T(2,128)(2,1)S(1)} %collective-permute-done), channel_id=1, source_target_pairs={{0,4},{4,8},{8,12},{12,0},{1,5},{5,9},{9,13},{13,1},{2,6},{6,10},{... | collective-permute-start | bytes 21512 | tf_op jit(solution)/shard_map/ppermute | solution.py:16
  14.7 6.0 %copy-start.3 = (u32[32]{0:T(128)S(1)}, u32[32]{0:T(128)}, u32[]{:S(2)}) copy-start(u32[32]{0:T(128)} %constant.67) | copy-start | bytes 388
  14.7 7.2 %copy-start.1 = (bf16[2,1792]{1,0:T(2,128)(2,1)S(1)}, bf16[2,1792]{1,0:T(2,128)(2,1)}, u32[]{:S(2)}) copy-start(bf16[2,1792]{1,0:T(2,128)(2,1)} %param.8) | copy-start | bytes 21508
  20.6 4.7 %copy-start.2 = (f32[14]{0:T(128)S(1)}, f32[14]{0:T(128)}, u32[]{:S(2)}) copy-start(f32[14]{0:T(128)} %param.11) | copy-start | bytes 172
  26.5 10.7 %all-to-all-start.1 = ((f32[1,8,14]{2,0,1:T(1,128)}), f32[1,8,14]{2,0,1:T(1,128)S(1)}, u32[]{:S(2)}, u32[]{:S(2)}) async-start(f32[1,8,14]{2,0,1:T(1,128)} %copy.54), calls=%async_computation.1 | async-start | bytes 8192 | tf_op jit(solution)/shard_map/all_to_all | solution.py:61
  37.1 9.0 %all-to-all-start.2 = ((f32[1,8,14]{2,0,1:T(1,128)}), f32[1,8,14]{2,0,1:T(1,128)S(1)}, u32[]{:S(2)}, u32[]{:S(2)}) async-start(f32[1,8,14]{2,0,1:T(1,128)} %copy.57), calls=%async_computation.2 | async-start | bytes 8192 | tf_op jit(solution)/shard_map/all_to_all | solution.py:62
  46.1 9.0 %all-to-all-start = ((f32[1,8,14,128]{3,0,2,1:T(1,128)}), f32[1,8,14,128]{3,0,2,1:T(1,128)S(1)}, u32[]{:S(2)}, u32[]{:S(2)}) async-start(f32[1,8,14,128]{3,0,2,1:T(1,128)} %copy.51), calls=%async_computation | async-start | bytes 114688 | tf_op jit(solution)/shard_map/all_to_all | solution.py:63
